TPU v7x, 32 devices: a whole 2x2x4 slice. The times are simulated.
32 devices in a mesh: rep: 2 (over y), gx: 4 (over x, core), gy: 4 (over z).
Axes of the slice: x: 2, y: 2, z: 4, core: 2. Of those that a mesh axis runs over, the one named last changes fastest.
Arguments:
- deltas: bfloat16 [2, 2, 3584, 14336], P('rep', None, 'gx', 'gy'), may hold values from -32 to 32
- params: float32 [2, 4, 4, 2, 4, 4, 112, 896], P(None, None, 'gx', 'rep', None, 'gy'), may hold values from -0.75 to 0.75
- momentum: float32 [2, 4, 4, 2, 4, 4, 112, 896], P(None, None, 'gx', 'rep', None, 'gy'), may hold values from -1.5 to 1.5
Outputs:
- new_params: float32 [2, 4, 4, 2, 4, 4, 112, 896], P(None, None, 'gx', 'rep', None, 'gy')
- new_momentum: float32 [2, 4, 4, 2, 4, 4, 112, 896], P(None, None, 'gx', 'rep', None, 'gy')
All inputs are finite; a program needn't handle non-finite values.
Results may differ from a plain program's by a relative error of at most 0.0003.
Values may be sent and summed in bfloat16 or wider, within the bound.
A program may use at most 128 MiB of HBM per device.

v0:
```python
import jax
import jax.numpy as jnp
from jax import lax
from jax.sharding import PartitionSpec as P

clip_level = 0.25
moment_decay = 0.9
outer_rate = 0.7
epsilon = 1e-06


def per_device(deltas, params, momentum):
    rows_split = lax.axis_size("gx")
    cols_split = lax.axis_size("gy")
    replicas = lax.axis_size("rep")
    matrices = deltas.shape[1]
    local_rows = deltas.shape[2]
    local_cols = deltas.shape[3]
    row_tile = local_rows // (rows_split * replicas)
    col_tile = local_cols // cols_split
    entries = matrices * local_rows * local_cols * rows_split * cols_split
    blocks = deltas.reshape(matrices, rows_split, replicas, row_tile, cols_split, col_tile)
    received = lax.all_to_all(blocks[None], "rep", split_axis=3, concat_axis=0, tiled=True)
    summed = jnp.sum(received, axis=0, dtype=jnp.float32)
    partial_value = summed / replicas
    squares = lax.psum(jnp.sum(partial_value * partial_value), ("rep", "gx", "gy"))
    mean_delta = lax.all_to_all(
        lax.all_to_all(partial_value, "gx", split_axis=1, concat_axis=1, tiled=True),
        "gy",
        split_axis=4,
        concat_axis=4,
        tiled=True,
    )
    root_mean = jnp.sqrt(squares / entries + epsilon)
    clip_scale = jnp.minimum(1.0, clip_level / root_mean)
    arranged = jnp.transpose(mean_delta, (0, 1, 2, 4, 3, 5)).reshape(params.shape)
    gradient = clip_scale * arranged
    new_momentum = moment_decay * momentum + gradient
    new_params = params - outer_rate * (gradient + moment_decay * new_momentum)
    return (new_params, new_momentum)


def solution(mesh):
    return jax.shard_map(
        per_device,
        mesh=mesh,
        in_specs=(
            P("rep", None, "gx", "gy"),
            P(None, None, "gx", "rep", None, "gy", None, None),
            P(None, None, "gx", "rep", None, "gy", None, None),
        ),
        out_specs=(
            P(None, None, "gx", "rep", None, "gy", None, None),
            P(None, None, "gx", "rep", None, "gy", None, None),
        ),
        check_vma=False,
    )
```

profile of v0, /device:TPU:0, one launch (start us, length us, event | category | flops | bytes accessed | tf_op | source)
XLA Modules:
  0.0 728.3 jit_solution(14214572394206877874)
XLA Ops:
  0.6 21.9 %broadcast_in_dim_reshape.3 = bf16[1,2,4,2,112,4,896]{6,5,4,3,2,1,0:T(4,128)(2,1)} reshape(bf16[1,2,896,3584]{3,2,1,0:T(8,128)(2,1)} %param.3) | data formatting | bytes 25690112 | tf_op jit(solution)/shard_map/broadcast_in_dim;reshape | solution.py:23
  22.6 7.8 %copy.20 = bf16[1,2,4,2,112,4,896]{6,5,4,2,1,0,3:T(4,128)(2,1)S(1)} copy(bf16[1,2,4,2,112,4,896]{6,5,4,3,2,1,0:T(4,128)(2,1)} %broadcast_in_dim_reshape.3) | data formatting | bytes 25690112 | tf_op jit(solution)/shard_map/broadcast_in_dim;reshape | solution.py:23
  30.4 146.6 %all_to_all.19 = bf16[1,2,4,2,112,4,896]{6,5,4,2,1,0,3:T(4,128)(2,1)} all-to-all(bf16[1,2,4,2,112,4,896]{6,5,4,2,1,0,3:T(4,128)(2,1)S(1)} %copy.20), channel_id=1, replica_groups=mesh['rep'=2,'gx'=4,'gy'=4] {'rep'}, dimensions={3} | all-to-all | bytes 25690112 | tf_op jit(solution)/shard_map/all_to_all | solution.py:23
  177.0 15.0 %convert_reduce_fusion = f32[2,4,112,4,896]{4,2,3,1,0:T(8,128)} fusion(bf16[1,2,4,2,112,4,896]{6,5,4,2,1,0,3:T(4,128)(2,1)} %all_to_all.19), kind=kLoop, calls=%fused_computation | loop fusion | flops 9633792 | bytes 25690112 | tf_op jit(solution)/shard_map/reduce_sum | solution.py:24
  192.1 15.7 %multiply_reduce_fusion = (f32[]{:T(128)}, f32[2,4,1,112,4,896]{5,4,3,1,0,2:T(4,128)}) fusion(f32[2,4,112,4,896]{4,2,3,1,0:T(8,128)} %convert_reduce_fusion), kind=kLoop, calls=%fused_computation.7 | loop fusion | flops 9633791 | bytes 25690116 | tf_op jit(solution)/shard_map/reduce_sum | solution.py:26
  207.8 10.6 %copy.23 = f32[2,4,1,112,4,896]{5,3,4,0,2,1:T(8,128)} copy(f32[2,4,1,112,4,896]{5,4,3,1,0,2:T(4,128)} %get-tuple-element.11) | data formatting | bytes 25690112 | tf_op jit(solution)/shard_map/div | solution.py:25
  218.5 150.4 %all_to_all.20 = f32[2,4,1,112,4,896]{5,3,4,0,2,1:T(8,128)} all-to-all(f32[2,4,1,112,4,896]{5,3,4,0,2,1:T(8,128)} %copy.23), channel_id=1, replica_groups=mesh['rep'=2,'gx'=4,'gy'=4] {'gx'}, dimensions={1} | all-to-all | bytes 25690112 | tf_op jit(solution)/shard_map/all_to_all | solution.py:28
  368.9 10.6 %copy.24 = f32[2,4,1,112,4,896]{5,3,1,0,2,4:T(8,128)} copy(f32[2,4,1,112,4,896]{5,3,4,0,2,1:T(8,128)} %all_to_all.20) | data formatting | bytes 25690112 | tf_op jit(solution)/shard_map/all_to_all | solution.py:28
  379.5 6.4 all-to-all-start.2
  385.9 298.0 %psum.7 = f32[]{:T(128)} all-reduce(f32[]{:T(128)} %get-tuple-element.10), channel_id=1, replica_groups=mesh['rep'=2,'gx'=4,'gy'=4] {'rep','gx','gy'}, use_global_device_ids=true, to_apply=%region_2.0 | all-reduce | flops 1 | bytes 8 | tf_op jit(solution)/shard_map/psum | solution.py:26
  684.6 0.0 all-to-all-done.2
  684.6 22.3 %bitcast_add_fusion.1 = (f32[2,4,1,1,4,1,112,896]{7,6,1,0,4,5,3,2:T(8,128)}, f32[2,4,1,1,4,1,112,896]{7,6,1,0,4,5,3,2:T(8,128)}) fusion(f32[2,4,1,1,4,1,112,896]{7,6,5,4,3,2,1,0:T(8,128)} %param.5, f32[2,4,1,112,4,896]{5,3,1,0,2,4:T(8,128)} %all-to-all-done.2, f32[]{:T(128)S(6)} %min_shard_map.3, f32[2,4,1,1,4,1,112,896]{7,6,5,4,3,2,1,0:T(8,128)} %param.4), kind=kLoop, calls=%fused_computation.3 | loop fusion | flops 22478848 | bytes 64225284 | tf_op jit(solution)/shard_map/add | solution.py:38
  706.9 10.7 %copy.28 = f32[2,4,1,1,4,1,112,896]{7,6,5,4,3,2,1,0:T(8,128)} copy(f32[2,4,1,1,4,1,112,896]{7,6,1,0,4,5,3,2:T(8,128)} %get-tuple-element.8) | data formatting | bytes 25690112
  717.6 10.7 %copy.27 = f32[2,4,1,1,4,1,112,896]{7,6,5,4,3,2,1,0:T(8,128)} copy(f32[2,4,1,1,4,1,112,896]{7,6,1,0,4,5,3,2:T(8,128)} %get-tuple-element.9) | data formatting | bytes 25690112
Async XLA Ops:
  379.5 305.1 %all-to-all-start.2 = ((f32[2,4,1,112,4,896]{5,3,1,0,2,4:T(8,128)}), f32[2,4,1,112,4,896]{5,3,1,0,2,4:T(8,128)}, u32[]{:S(2)}, u32[]{:S(2)}) async-start(f32[2,4,1,112,4,896]{5,3,1,0,2,4:T(8,128)} %copy.24), calls=%async_computation.2 | async-start | bytes 25690112 | tf_op jit(solution)/shard_map/all_to_all | solution.py:27
where the time goes:
time: 730 us; the launch traced here: 728 us
  blocking collectives  595 us (82%)
  local copies, waits for them, and re-layouts  72.4 us (10%)
  other arithmetic  53.1 us (7%)
    psum x1, blocking collectives, per_device(): lax.psum(jnp.sum(partial_value * partial_value), ('rep', 'gx', 'gy'))  298 us
    all_to_all x1, blocking collectives, per_device(): lax.all_to_all(partial_value, 'gx', split_axis=1, concat_axis=1, tiled=True)  150 us
    all_to_all x1, blocking collectives, per_device(): lax.all_to_all(blocks[None], 'rep', split_axis=3, concat_axis=0, tiled=True)  147 us
    another operation x2, local copies, waits for them, and re-layouts, per_device(): blocks[None]  29.8 us
    add x1, other arithmetic, per_device(): new_momentum = moment_decay * momentum + gradient  22.3 us
    unnamed x2, local copies, waits for them, and re-layouts  21.4 us
    reduce_sum x1, other arithmetic, per_device(): jnp.sum(partial_value * partial_value)  15.7 us
    reduce_sum x1, other arithmetic, per_device(): summed = jnp.sum(received, axis=0, dtype=jnp.float32)  15 us
  transfers between devices with their start and end apart: 1, of which 0 were waited for; matrix products, arithmetic and copies ran while one was open for 0% of the time, Pallas kernels for 0%

commit v1 on v0

--- a/solution.py
+++ b/solution.py
@@ -25,7 +25,12 @@
     partial_value = summed / replicas
     squares = lax.psum(jnp.sum(partial_value * partial_value), ("rep", "gx", "gy"))
     mean_delta = lax.all_to_all(
-        lax.all_to_all(partial_value, "gx", split_axis=1, concat_axis=1, tiled=True),
+        jnp.concatenate(
+            lax.all_to_all(
+                jnp.stack(jnp.split(partial_value, lax.axis_size("gx"), axis=1)), "gx", 0, 0
+            ),
+            axis=1,
+        ),
         "gy",
         split_axis=4,
         concat_axis=4,

time: 730 us -> 735 us (level)
    another operation x0 -> x2, local copies, waits for them, and re-layouts: none -> 12.9 us  [per_device(): jnp.stack(jnp.split(partial_value, lax.axis_size('gx'), axis=1))]
    div x1 -> x0, local copies, waits for them, and re-layouts: 10.6 us -> none  [per_device(): partial_value = summed / replicas]
    all_to_all x1 -> x0, local copies, waits for them, and re-layouts: 10.6 us -> none  [per_device(): lax.all_to_all(partial_value, 'gx', split_axis=1, concat_axis=1, tiled=True)]
    reshape x0 -> x1, local copies, waits for them, and re-layouts: none -> 10.6 us  [per_device(): jnp.concatenate(lax.all_to_all(jnp.stack(jnp.split(partial_value, lax.axi...]
where the time goes in v1:
time: 735 us; the launch traced here: 734 us
  blocking collectives  595 us (81%)
  local copies, waits for them, and re-layouts  74.7 us (10%)
  other arithmetic  56.2 us (8%)
    psum x1, blocking collectives, per_device(): lax.psum(jnp.sum(partial_value * partial_value), ('rep', 'gx', 'gy'))  298 us
    all_to_all x1, blocking collectives, per_device(): lax.all_to_all(jnp.stack(jnp.split(partial_value, lax.axis_size('gx'), ax...  150 us
    all_to_all x1, blocking collectives, per_device(): lax.all_to_all(blocks[None], 'rep', split_axis=3, concat_axis=0, tiled=True)  147 us
    another operation x2, local copies, waits for them, and re-layouts, per_device(): blocks[None]  29.8 us
    add x1, other arithmetic, per_device(): new_momentum = moment_decay * momentum + gradient  22.3 us
    unnamed x2, local copies, waits for them, and re-layouts  21.4 us
    reduce_sum x1, other arithmetic, per_device(): summed = jnp.sum(received, axis=0, dtype=jnp.float32)  15 us
  transfers between devices with their start and end apart: 1, of which 0 were waited for; matrix products, arithmetic and copies ran while one was open for 0% of the time, Pallas kernels for 0%

profile of v1, /device:TPU:0, one launch (start us, length us, event | category | flops | bytes accessed | tf_op | source)
XLA Modules:
  0.0 733.7 jit_solution(11662160768231156437)
XLA Ops:
  0.6 21.9 %broadcast_in_dim_reshape.3 = bf16[1,2,4,2,112,4,896]{6,5,4,3,2,1,0:T(4,128)(2,1)} reshape(bf16[1,2,896,3584]{3,2,1,0:T(8,128)(2,1)} %param.3) | data formatting | bytes 25690112 | tf_op jit(solution)/shard_map/broadcast_in_dim;reshape | solution.py:23
  22.6 7.8 %copy.29 = bf16[1,2,4,2,112,4,896]{6,5,4,2,1,0,3:T(4,128)(2,1)S(1)} copy(bf16[1,2,4,2,112,4,896]{6,5,4,3,2,1,0:T(4,128)(2,1)} %broadcast_in_dim_reshape.3) | data formatting | bytes 25690112 | tf_op jit(solution)/shard_map/broadcast_in_dim;reshape | solution.py:23
  30.4 146.6 %all_to_all.19 = bf16[1,2,4,2,112,4,896]{6,5,4,2,1,0,3:T(4,128)(2,1)} all-to-all(bf16[1,2,4,2,112,4,896]{6,5,4,2,1,0,3:T(4,128)(2,1)S(1)} %copy.29), channel_id=1, replica_groups=mesh['rep'=2,'gx'=4,'gy'=4] {'rep'}, dimensions={3} | all-to-all | bytes 25690112 | tf_op jit(solution)/shard_map/all_to_all | solution.py:23
  177.0 15.0 %convert_reduce_fusion = f32[2,4,112,4,896]{4,2,3,1,0:T(8,128)} fusion(bf16[1,2,4,2,112,4,896]{6,5,4,2,1,0,3:T(4,128)(2,1)} %all_to_all.19), kind=kLoop, calls=%fused_computation | loop fusion | flops 9633792 | bytes 25690112 | tf_op jit(solution)/shard_map/reduce_sum | solution.py:24
  192.1 12.6 %multiply_reduce_fusion = (f32[]{:T(128)}, f32[2,4,1,112,4,896]{5,4,3,1,0,2:T(4,128)S(1)}) fusion(f32[2,4,112,4,896]{4,2,3,1,0:T(8,128)} %convert_reduce_fusion), kind=kLoop, calls=%fused_computation.8 | loop fusion | flops 9633791 | bytes 25690116 | tf_op jit(solution)/shard_map/reduce_sum | solution.py:26
  204.7 2.2 slice_bitcast_fusion.3
  206.9 6.3 pad_maximum_fusion
  213.2 10.6 %copy.35 = f32[4,2,1,1,112,4,896]{6,4,5,1,3,2,0:T(8,128)} copy(f32[4,2,1,1,112,4,896]{6,5,4,1,3,2,0:T(4,128)} %pad_maximum_fusion) | data formatting | bytes 25690112 | tf_op jit(solution)/shard_map/stack | solution.py:30
  223.9 150.4 %all_to_all.20 = f32[4,2,1,1,112,4,896]{6,4,5,1,3,2,0:T(8,128)} all-to-all(f32[4,2,1,1,112,4,896]{6,4,5,1,3,2,0:T(8,128)} %copy.35), channel_id=1, replica_groups=mesh['rep'=2,'gx'=4,'gy'=4] {'gx'}, dimensions={0} | all-to-all | bytes 25690112 | tf_op jit(solution)/shard_map/all_to_all | solution.py:29
  374.3 10.6 %copy.36 = f32[2,4,1,112,4,896]{5,3,1,0,2,4:T(8,128)} copy(f32[2,4,1,112,4,896]{5,3,4,0,1,2:T(8,128)} %bitcast.32) | data formatting | bytes 25690112 | tf_op jit(solution)/shard_map/reshape | solution.py:28
  384.9 6.4 all-to-all-start.2
  391.3 298.0 %psum.7 = f32[]{:T(128)} all-reduce(f32[]{:T(128)} %get-tuple-element.10), channel_id=1, replica_groups=mesh['rep'=2,'gx'=4,'gy'=4] {'rep','gx','gy'}, use_global_device_ids=true, to_apply=%region_2.0 | all-reduce | flops 1 | bytes 8 | tf_op jit(solution)/shard_map/psum | solution.py:26
  690.0 0.0 all-to-all-done.2
  690.0 22.3 %bitcast_add_fusion.1 = (f32[2,4,1,1,4,1,112,896]{7,6,1,0,4,5,3,2:T(8,128)}, f32[2,4,1,1,4,1,112,896]{7,6,1,0,4,5,3,2:T(8,128)}) fusion(f32[2,4,1,1,4,1,112,896]{7,6,5,4,3,2,1,0:T(8,128)} %param.5, f32[2,4,1,112,4,896]{5,3,1,0,2,4:T(8,128)} %all-to-all-done.2, f32[]{:T(128)S(6)} %min_shard_map.3, f32[2,4,1,1,4,1,112,896]{7,6,5,4,3,2,1,0:T(8,128)} %param.4), kind=kLoop, calls=%fused_computation.4 | loop fusion | flops 22478848 | bytes 64225284 | tf_op jit(solution)/shard_map/add | solution.py:43
  712.3 10.7 %copy.40 = f32[2,4,1,1,4,1,112,896]{7,6,5,4,3,2,1,0:T(8,128)} copy(f32[2,4,1,1,4,1,112,896]{7,6,1,0,4,5,3,2:T(8,128)} %get-tuple-element.8) | data formatting | bytes 25690112
  723.0 10.7 %copy.39 = f32[2,4,1,1,4,1,112,896]{7,6,5,4,3,2,1,0:T(8,128)} copy(f32[2,4,1,1,4,1,112,896]{7,6,1,0,4,5,3,2:T(8,128)} %get-tuple-element.9) | data formatting | bytes 25690112
Async XLA Ops:
  384.9 305.1 %all-to-all-start.2 = ((f32[2,4,1,112,4,896]{5,3,1,0,2,4:T(8,128)}), f32[2,4,1,112,4,896]{5,3,1,0,2,4:T(8,128)}, u32[]{:S(2)}, u32[]{:S(2)}) async-start(f32[2,4,1,112,4,896]{5,3,1,0,2,4:T(8,128)} %copy.36), calls=%async_computation.2 | async-start | bytes 25690112 | tf_op jit(solution)/shard_map/all_to_all | solution.py:27
